TPU v7x, 128 devices: a whole 4x4x4 slice. The times are simulated.
128 devices in a mesh: gx: 4 (over x_lo, core), gy: 4 (over y), gz: 8 (over x_hi, z).
Axes of the slice: x: 4 (x_hi: 2, x_lo: 2; x = x_hi * 2 + x_lo), y: 4, z: 4, core: 2. Of those that a mesh axis runs over, the one named last changes fastest.
Arguments:
- inv_factor: bfloat16 [4, 4, 8, 1536, 1536], P('gx', 'gy', 'gz'), as said below
- coupling: bfloat16 [4, 4, 8, 1536, 1536], P('gx', 'gy', 'gz'), may hold values from -0.15625 to 0.15625
- stiff_gg: bfloat16 [4, 4, 8, 1536, 1536], P('gx', 'gy', 'gz'), as said below
- block_order: int32 [4, 4, 8, 12], P('gx', 'gy', 'gz'), may hold values from 0 to 11, each once within a row
Outputs:
- assembled: float32 [4, 4, 8, 1536, 1536], P('gx', 'gy', 'gz')
Inputs may be any that keep to these rules, and one draw needn't show every extreme that they name: `block_order`: each subdomain's row is a permutation of 0 to 11. `stiff_gg`: each subdomain's block is symmetric. `inv_factor`: each subdomain's block is lower triangular with a positive diagonal.
All inputs are finite; a program needn't handle non-finite values.
Results may differ from a plain program's by a relative error of at most 0.0016.
Values sent between devices are 32-bit elements; how exact they have to be, the bound alone decides.
No kernel may reach another device: no remote copies, remote signals or barrier semaphores. Data moves between devices by JAX's collectives and lax.ppermute only.
A program may use at most 128 MiB of HBM per device.

v0:
```python
import jax
import jax.numpy as jnp
from jax import lax
from jax.experimental import pallas as pl
from jax.experimental.pallas import tpu as pltpu
from jax.sharding import PartitionSpec as P


BLK = 128
NBLK = 12
PAN = 256

PAIRS = {"A": (4, 5), "B": (8, 9), "C": (6, 7), "D": (10, 11), "E": (2, 3), "F": (0, 1)}
COLUMNS = (8, 9, 10, 11, 4, 5, 6, 7, 2, 3, 0, 1)
Z_HIGH, Z_LOW = ((6, 7), (6, 10), (6, 11), (7, 10), (7, 11), (10, 11)), ((4, 5), (4, 8), (4, 9), (5, 8), (5, 9), (8, 9))
Z_HIGH_PACK, Z_LOW_PACK = ((6, 7), (11, 10)), ((4, 5), (8, 9))
Y_HIGH, Y_LOW = ((3, 3), (3, 9), (3, 11), (9, 11)), ((2, 2), (2, 8), (2, 10), (8, 10))
KEPT = ((2, 3), (2, 9), (3, 8), (2, 11), (3, 10), (8, 11), (9, 10), (0, 1))
FACES = 8 * BLK
GROUPS = ((0, 2), (2, 4), (4, 6))
MESSAGE = FACES + 8


def position(order, k):
    if k < 2:
        at = k ^ (lax.axis_index("gx") % 2)
    elif k < 4:
        at = 2 + ((k - 2) ^ (lax.axis_index("gy") % 2))
    elif k < 8:
        at = 4 + ((k - 4) ^ (2 * (lax.axis_index("gz") % 2)))
    else:
        at = 8 + ((k - 8) ^ (lax.axis_index("gy") % 2 + 2 * (lax.axis_index("gz") % 2)))
    return pl.multiple_of(order[at] * BLK, BLK)


def positions(order):
    return [position(order, k) for k in range(NBLK)]


def fetch_order(order, osmem, sem):
    copy = pltpu.make_async_copy(order, osmem, sem)
    copy.start()
    return copy


def stiff_copies(at, stiff, buf, sem, blocks):
    return [
        pltpu.make_async_copy(
            stiff.at[pl.ds(at[k], BLK), pl.ds(at[l], BLK)], buf.at[pl.ds(n * BLK, BLK), :], sem
        )
        for n, (k, l) in enumerate(blocks)
    ]


def weigh(lbuf, cbuf, columns, pan):
    depth = (pan + 1) * PAN
    return jnp.dot(
        lbuf[pan * PAN : depth, :depth], cbuf[:depth, columns], preferred_element_type=jnp.float32
    ).astype(jnp.bfloat16)


def gram(left, right):
    return lax.dot_general(left, right, (((0,), (0,)), ((), ())), preferred_element_type=jnp.float32)


def rows_ge():
    r = lax.broadcasted_iota(jnp.int32, (BLK, BLK), 0)
    c = lax.broadcasted_iota(jnp.int32, (BLK, BLK), 1)
    return r, c


def pack(first, second):
    r, c = rows_ge()
    return jnp.where(r <= c, first, second), jnp.sum(jnp.where(r == c, second, 0.0), axis=0, keepdims=True)


def unpack(tile, diagonal):
    r, c = rows_ge()
    turned = tile.T
    first = jnp.where(r <= c, tile, turned)
    return first, jnp.where(r > c, tile, jnp.where(r < c, turned, diagonal))


def two_rows(first, second):
    row = lax.broadcasted_iota(jnp.int32, (8, BLK), 0)
    return jnp.where(row == 0, first, jnp.where(row == 1, second, 0.0))


def piece(result, i, j):
    return result[i * BLK : (i + 1) * BLK, j * BLK : (j + 1) * BLK]


def slot(n):
    return slice(n * BLK, (n + 1) * BLK)


FACE_BLOCKS = ((4, 4), (4, 5), (5, 5), (4, 8), (4, 9), (5, 8), (5, 9), (6, 6), (6, 7), (7, 7), (6, 10), (6, 11), (7, 10), (7, 11))
SIDE_BLOCKS = tuple((k, l) for k in (2, 3) for l in (2, 3, 8, 9, 10, 11) if k <= l) + ((8, 10), (8, 11), (9, 10), (9, 11), (0, 0), (0, 1), (1, 1))
REST = (
    ("F", (("bd", (8, 9, 10, 11)), ("ac", (4, 5, 6, 7)), ("e", (2, 3)))),
    ("E", (("ac", (4, 5, 6, 7)),)),
    ("A", (("c", (6, 7)), ("d", (10, 11)))),
    ("C", (("b", (8, 9)),)),
)
REST_BLOCKS = tuple((k, l) for left, rights in REST for _, cols in rights for k in PAIRS[left] for l in cols)
LATER = FACE_BLOCKS + SIDE_BLOCKS + REST_BLOCKS
AT_FACES, AT_SIDES, AT_REST = 0, len(FACE_BLOCKS), len(FACE_BLOCKS) + len(SIDE_BLOCKS)
EDGE_BLOCKS = ((8, 8), (8, 9), (9, 9), (10, 10), (10, 11), (11, 11))


def edge_kernel(order, inverse, coupling, stiff, lbuf, cbuf, sall, wbd, yda, ydb, zpart, spots, osmem, sbuf, osem, lsem, csem, rsem, ssem):
    fetch = fetch_order(order, osmem, osem)
    panels = lbuf.shape[0] // PAN
    lcopies = [
        pltpu.make_async_copy(
            inverse.at[pl.ds(pan * PAN, PAN), pl.ds(0, (pan + 1) * PAN)],
            lbuf.at[pl.ds(pan * PAN, PAN), pl.ds(0, (pan + 1) * PAN)],
            lsem.at[pan],
        )
        for pan in range(panels)
    ]
    for copy in lcopies:
        copy.start()
    fetch.wait()
    at = positions(osmem)
    lane = lax.broadcasted_iota(jnp.int32, (8, BLK), 1)
    spots[...] = sum(jnp.where(lane == k, at[k], 0) for k in range(NBLK))
    ccopies = []
    for lo, hi in GROUPS:
        rows = pl.ds(lo * PAN, (hi - lo) * PAN)
        group = [
            pltpu.make_async_copy(
                coupling.at[rows, pl.ds(at[k], BLK)], cbuf.at[rows, pl.ds(n * BLK, BLK)], csem.at[lo]
            )
            for n, k in enumerate(COLUMNS[:4])
        ]
        ccopies.append(group)
        for copy in group:
            copy.start()
    scopies = stiff_copies(at, stiff, sbuf, ssem, EDGE_BLOCKS)
    for copy in scopies:
        copy.start()
    later = [
        pltpu.make_async_copy(
            coupling.at[:, pl.ds(at[k], BLK)], cbuf.at[:, pl.ds((n + 4) * BLK, BLK)], rsem
        )
        for n, k in enumerate(COLUMNS[4:])
    ]
    later += stiff_copies(at, stiff, sall, rsem, LATER)
    for (lo, hi), group in zip(GROUPS, ccopies):
        for pan in range(lo, hi):
            lcopies[pan].wait()
        for copy in group:
            copy.wait()
        if lo == 0:
            for copy in later:
                copy.start()
        for pan in range(lo, hi):
            wbd[pan * PAN : (pan + 1) * PAN, :] = weigh(lbuf, cbuf, slice(0, 512), pan)
    for copy in scopies:
        copy.wait()
    full = []
    for n in range(2):
        half = wbd[:, n * 256 : (n + 1) * 256]
        result = gram(half, half)
        for m, (i, j) in enumerate(((0, 0), (0, 1), (1, 1))):
            full.append(sbuf[slot(n * 3 + m)].astype(jnp.float32) - piece(result, i, j))
    b8, b89, b9, b10, b1011, b11 = full
    ydb[:BLK], row = pack(b8, b10)
    ydb[BLK:] = two_rows(row, 0.0)
    yda[:BLK], row = pack(b11, b9)
    yda[BLK:] = two_rows(row, 0.0)
    zpart[slot(0)] = b89
    zpart[slot(1)] = b1011
    zpart[slot(2)], low = pack(b8, b9)
    zpart[slot(3)], high = pack(b11, b10)
    zpart[4 * BLK :] = two_rows(low, high)
    for copy in later:
        copy.wait()


def face_kernel(sall, lbuf, cbuf, wbd, zpart, wac, za, zb):
    for pan in range(lbuf.shape[0] // PAN):
        wac[pan * PAN : (pan + 1) * PAN, :] = weigh(lbuf, cbuf, slice(512, 1024), pan)
    for n, (out, part) in enumerate(((zb, 0), (za, 1))):
        own = wac[:, n * 256 : (n + 1) * 256]
        inner = gram(own, own)
        outer = gram(own, wbd[:, n * 256 : (n + 1) * 256])
        base = AT_FACES + n * 7

        def value(m, result, i, j):
            return sall[slot(base + m)].astype(jnp.float32) - piece(result, i, j)

        out[slot(6)], row = pack(value(0, inner, 0, 0), value(2, inner, 1, 1))
        out[slot(0)] = value(1, inner, 0, 1)
        for m, (i, j) in enumerate(((0, 0), (0, 1), (1, 0), (1, 1))):
            out[slot(1 + m)] = value(3 + m, outer, i, j)
        out[slot(5)] = zpart[slot(part)]
        out[slot(7)] = zpart[slot(2 + part)]
        out[FACES:] = two_rows(row, zpart[4 * BLK + part : 4 * BLK + part + 1])


def join_kernel(za, zb, fya, fyb, za_out, zb_out):
    del za, zb
    r, c = rows_ge()
    above = r <= c
    row = lax.broadcasted_iota(jnp.int32, (8, BLK), 0) == 1
    below, diagonal = known("gy", fyb[:BLK]), known("gy", fyb[BLK : BLK + 1])
    za_out[slot(7)] = za_out[slot(7)] + jnp.where(above, fya[:BLK], below)
    za_out[FACES:] = za_out[FACES:] + jnp.where(row, diagonal, 0.0)
    zb_out[slot(7)] = zb_out[slot(7)] + jnp.where(above, below, fya[:BLK])
    zb_out[FACES:] = zb_out[FACES:] + jnp.where(row, fya[BLK : BLK + 1], 0.0)


def side_kernel(sall, lbuf, cbuf, wbd, after, wef, yea, yeb, xa, xb, keep):
    del after
    for pan in range(lbuf.shape[0] // PAN):
        wef[pan * PAN : (pan + 1) * PAN, :] = weigh(lbuf, cbuf, slice(1024, 1536), pan)
    e, f = wef[:, :256], wef[:, 256:]
    targets = {pair: (yea, n) for n, pair in enumerate(Y_HIGH)} | {pair: (yeb, n) for n, pair in enumerate(Y_LOW)}
    targets |= {pair: (keep, n) for n, pair in enumerate(KEPT)} | {(1, 1): (xa, 0), (0, 0): (xb, 0)}

    def emit(result, rows, cols):
        for i, k in enumerate(rows):
            for j, l in enumerate(cols):
                if k <= l:
                    out, n = targets[(k, l)]
                    m = AT_SIDES + SIDE_BLOCKS.index((k, l))
                    out[slot(n)] = sall[slot(m)].astype(jnp.float32) - piece(result, i, j)

    emit(gram(e, e), (2, 3), (2, 3))
    emit(gram(e, wbd[...]), (2, 3), (8, 9, 10, 11))
    emit(gram(wbd[:, :256], wbd[:, 256:]), (8, 9), (10, 11))
    emit(gram(f, f), (0, 1), (0, 1))


class Writer:
    def __init__(self, spots, out, stage, sem):
        row = spots[0:1, :]
        self.at = [pl.multiple_of(row[0, k], BLK) for k in range(NBLK)]
        self.out, self.stage, self.sem, self.copies = out, stage, sem, []

    def put(self, k, l, value):
        n = len(self.copies)
        self.stage[slot(n)] = value
        copy = pltpu.make_async_copy(
            self.stage.at[pl.ds(n * BLK, BLK), :],
            self.out.at[pl.ds(self.at[k], BLK), pl.ds(self.at[l], BLK)],
            self.sem,
        )
        copy.start()
        self.copies.append(copy)

    def emit(self, k, l, value):
        self.put(k, l, value)
        if k != l:
            self.put(l, k, value.T)

    def finish(self):
        for copy in self.copies:
            copy.wait()


def rest_kernel(spots, sall, wbd, wac, wef, keep, out, turned, stage, wsem):
    writer = Writer(spots, out, stage, wsem)
    whole = {"ac": (wac, 0, 512), "bd": (wbd, 0, 512), "e": (wef, 0, 256), "f": (wef, 256, 512), "a": (wac, 0, 256)}
    whole |= {"c": (wac, 256, 512), "b": (wbd, 0, 256), "d": (wbd, 256, 512)}
    for n, (k, l) in enumerate(KEPT):
        writer.emit(k, l, keep[slot(n)])
    m = AT_REST
    for left, rights in REST:
        ref, lo, hi = whole[left.lower()]
        turned[...] = ref[:, lo:hi].T
        for name, cols in rights:
            ref, lo, hi = whole[name]
            result = jnp.dot(turned[...], ref[:, lo:hi], preferred_element_type=jnp.float32)
            for i, k in enumerate(PAIRS[left]):
                for j, l in enumerate(cols):
                    writer.emit(k, l, sall[slot(m)].astype(jnp.float32) - piece(result, i, j))
                    m += 1
    writer.finish()


def border_kernel(spots, yea, yeb, fyea, fyeb, before, out, stage, wsem):
    del before
    writer = Writer(spots, out, stage, wsem)
    for n, (k, l) in enumerate(Y_HIGH):
        writer.emit(k, l, yea[slot(n)] + fyea[slot(n)])
    for n, (k, l) in enumerate(Y_LOW):
        writer.emit(k, l, yeb[slot(n)] + known("gy", fyeb[slot(n)]))
    writer.finish()


def last_kernel(spots, za, zb, fza, fzb, xa, xb, fxa, fxb, before, out, stage, wsem):
    del before
    writer = Writer(spots, out, stage, wsem)
    for pairs, packs, own, other, take in (
        (Z_LOW, Z_LOW_PACK, zb, fzb, lambda value: known("gz", value)),
        (Z_HIGH, Z_HIGH_PACK, za, fza, lambda value: value),
    ):
        for n, (k, l) in enumerate(pairs):
            writer.emit(k, l, own[slot(n)] + take(other[slot(n)]))
        for n, (k, l) in enumerate(packs):
            row = slice(FACES + n, FACES + n + 1)
            first, second = unpack(own[slot(6 + n)] + take(other[slot(6 + n)]), own[row] + take(other[row]))
            writer.emit(k, k, first)
            writer.emit(l, l, second)
    writer.emit(0, 0, xb[...] + known("gx", fxb[...]))
    writer.emit(1, 1, xa[...] + fxa[...])
    writer.finish()


def exchange_high(value, axis):
    return lax.ppermute(value, axis, [(i, i ^ 1) for i in range(lax.axis_size(axis))])


def exchange_low(value, axis):
    size, across = lax.axis_size(axis), lax.axis_size("gx")
    if axis == "gx":
        return lax.ppermute(value, axis, [(i, size - 1 - i) for i in range(size)])
    pairs = []
    for x in range(across):
        for i in range(size):
            to = (x ^ 1, i) if i in (0, size - 1) else (x, ((i - 1) ^ 1) + 1)
            pairs.append((x * size + i, to[0] * size + to[1]))
    return lax.ppermute(value, ("gx", axis), pairs)


def known(axis, value):
    at = lax.axis_index(axis)
    return jnp.where((at > 0) & (at < lax.axis_size(axis) - 1), value, 0.0)


HBM = pl.BlockSpec(memory_space=pltpu.HBM)
VMEM = pl.BlockSpec(memory_space=pltpu.VMEM)
DMA = pltpu.SemaphoreType.DMA


def shape(*dims, dtype=jnp.float32):
    return jax.ShapeDtypeStruct(dims, dtype)


def params(mib):
    return pltpu.CompilerParams(vmem_limit_bytes=mib * 1024 * 1024)


def cost(gigaflops, megabytes):
    return pl.CostEstimate(
        flops=int(gigaflops * 1e9), bytes_accessed=int(megabytes * 1e6), transcendentals=0
    )


def in_hbm(value):
    return pltpu.with_memory_space_constraint(value, pltpu.HBM)


def shards(inv_factor, coupling, stiff_gg, block_order):
    rows = inv_factor.shape[3]
    size = NBLK * BLK
    half = jnp.bfloat16
    order = in_hbm(block_order.reshape(NBLK))
    inverse = in_hbm(inv_factor.reshape(rows, rows))
    coupled = in_hbm(coupling.reshape(rows, size))
    stiff = in_hbm(stiff_gg.reshape(size, size))
    panels = rows // PAN
    osmem = pltpu.SMEM((NBLK,), jnp.int32)

    lbuf, cbuf, sall, wbd, yda, ydb, zpart, spots = pl.pallas_call(
        edge_kernel,
        out_shape=(
            shape(rows, rows, dtype=half),
            shape(rows, size, dtype=half),
            shape(len(LATER) * BLK, BLK, dtype=half),
            shape(rows, 512, dtype=half),
            shape(BLK + 8, BLK),
            shape(BLK + 8, BLK),
            shape(4 * BLK + 8, BLK),
            shape(8, BLK, dtype=jnp.int32),
        ),
        in_specs=[HBM] * 4,
        out_specs=(VMEM,) * 8,
        scratch_shapes=[osmem, pltpu.VMEM((len(EDGE_BLOCKS) * BLK, BLK), half), DMA, DMA((panels,)), DMA((panels,)), DMA, DMA],
        compiler_params=params(12),
        cost_estimate=cost(3, 8),
        name="edges",
    )(order, inverse, coupled, stiff)
    fya = exchange_high(yda, "gy")
    fyb = exchange_low(ydb, "gy")
    wac, za, zb = pl.pallas_call(
        face_kernel,
        out_shape=(shape(rows, 512, dtype=half), shape(MESSAGE, BLK), shape(MESSAGE, BLK)),
        in_specs=[VMEM] * 5,
        out_specs=(VMEM,) * 3,
        compiler_params=params(12),
        cost_estimate=cost(3, 1),
        name="faces",
    )(sall, lbuf, cbuf, wbd, zpart)
    za, zb = pl.pallas_call(
        join_kernel,
        out_shape=(shape(MESSAGE, BLK), shape(MESSAGE, BLK)),
        in_specs=[VMEM] * 4,
        out_specs=(VMEM,) * 2,
        input_output_aliases={0: 0, 1: 1},
        compiler_params=params(2),
        cost_estimate=cost(0.1, 0.1),
        name="join",
    )(za, zb, fya, fyb)
    fzb = exchange_low(zb, "gz")
    fza = exchange_high(za, "gz")
    wef, yea, yeb, xa, xb, keep = pl.pallas_call(
        side_kernel,
        out_shape=(
            shape(rows, 512, dtype=half),
            shape(4 * BLK, BLK),
            shape(4 * BLK, BLK),
            shape(BLK, BLK),
            shape(BLK, BLK),
            shape(len(KEPT) * BLK, BLK),
        ),
        in_specs=[VMEM] * 5,
        out_specs=(VMEM,) * 6,
        compiler_params=params(12),
        cost_estimate=cost(3, 1),
        name="sides",
    )(sall, lbuf, cbuf, wbd, za)
    fyea = exchange_high(yea, "gy")
    fyeb = exchange_low(yeb, "gy")
    fxa = exchange_high(xa, "gx")
    fxb = exchange_low(xb, "gx")
    out = pl.pallas_call(
        rest_kernel,
        out_shape=shape(size, size),
        in_specs=[VMEM] * 6,
        out_specs=HBM,
        scratch_shapes=[
            pltpu.VMEM((PAN, rows), half),
            pltpu.VMEM((2 * (len(KEPT) + len(REST_BLOCKS)) * BLK, BLK), jnp.float32),
            DMA,
        ],
        compiler_params=params(16),
        cost_estimate=cost(3, 8),
        name="rest",
    )(spots, sall, wbd, wac, wef, keep)
    out = pl.pallas_call(
        border_kernel,
        out_shape=shape(size, size),
        in_specs=[VMEM] * 5 + [HBM],
        out_specs=HBM,
        scratch_shapes=[pltpu.VMEM((14 * BLK, BLK), jnp.float32), DMA],
        input_output_aliases={5: 0},
        compiler_params=params(4),
        cost_estimate=cost(0.1, 1),
        name="borders",
    )(spots, yea, yeb, fyea, fyeb, out)
    out = pl.pallas_call(
        last_kernel,
        out_shape=shape(size, size),
        in_specs=[VMEM] * 9 + [HBM],
        out_specs=HBM,
        scratch_shapes=[pltpu.VMEM((34 * BLK, BLK), jnp.float32), DMA],
        input_output_aliases={9: 0},
        compiler_params=params(8),
        cost_estimate=cost(0.1, 2),
        name="last",
    )(spots, za, zb, fza, fzb, xa, xb, fxa, fxb, out)
    return out.reshape(1, 1, 1, size, size)


def solution(mesh):
    return jax.shard_map(
        shards,
        mesh=mesh,
        in_specs=(
            P("gx", "gy", "gz", None, None),
            P("gx", "gy", "gz", None, None),
            P("gx", "gy", "gz", None, None),
            P("gx", "gy", "gz", None),
        ),
        out_specs=P("gx", "gy", "gz", None, None),
        check_vma=False,
    )
```

profile of v0, /device:TPU:4, one launch (start us, length us, event | category | flops | bytes accessed | tf_op | source)
XLA Modules:
  0.0 34.9 jit_solution(10478325525697376505)
XLA Ops:
  0.0 4.8 %edges.1 = (bf16[1536,1536]{1,0:T(8,128)(2,1)S(1)}, bf16[1536,1536]{1,0:T(8,128)(2,1)S(1)}, bf16[9216,128]{1,0:T(8,128)(2,1)S(1)}, bf16[1536,512]{1,0:T(8,128)(2...) custom-call(s32[12]{0:T(128)} %bitcast.8, ...), custom_call_target="tpu_custom_call" | custom-call | flops 3000000000 | bytes 8000000 | tf_op jit(solution)/shard_map/edges/pallas_call | solution.py:368
  4.8 1.7 %collective-permute-start = (f32[136,128]{1,0:T(8,128)S(1)}, f32[136,128]{1,0:T(8,128)S(1)}, u32[]{:S(2)}, u32[]{:S(2)}) collective-permute-start(f32[136,128]{1,0:T(8,128)S(1)} %get-tuple-element.32), channel_id=1, source_target_pairs={{0,8},{8,0},{16,24},{24,16},{1,9},{9,1},{17,25},{25,17},{2,10},{10... | collective-permute-start | bytes 208904 | tf_op jit(solution)/shard_map/ppermute | solution.py:314
  6.5 0.0 collective-permute-start.1
  6.5 2.5 %faces.1 = (bf16[1536,512]{1,0:T(8,128)(2,1)S(1)}, f32[1032,128]{1,0:T(8,128)S(1)}, f32[1032,128]{1,0:T(8,128)S(1)}) custom-call(bf16[9216,128]{1,0:T(8,128)(2,1)S(1)} %get-tuple-element.25.sall, bf16[1536,1536]{1,0:T(8,128)(2,1)S(1)} %get-tuple-element.26.lbuf, bf16[1536,1536]{1,0:T(8,128)(2,1)S(1)} %get-tuple-element.27.cbuf, ...), custom_call_target="tpu_custom_call" | custom-call | flops 3000000000 | bytes 1000000 | tf_op jit(solution)/shard_map/faces/pallas_call | solution.py:389
  8.9 0.3 collective-permute-done.fya
  9.2 0.0 collective-permute-done.1.fyb
  9.2 2.7 %sides.1 = (bf16[1536,512]{1,0:T(8,128)(2,1)S(1)}, f32[512,128]{1,0:T(8,128)S(1)}, f32[512,128]{1,0:T(8,128)S(1)}, f32[128,128]{1,0:T(8,128)S(1)}, f32[128,128]{1,0:T(8,128)S(1)}, /*index=5*/f32[1024,128]{1,0:T(8,128)S(1)}) custom-call(bf16[9216,128]{1,0:T(8,128)(2,1)S(1)} %get-tuple-element.25.sall, bf16[1536,1536]{1,0:T(8,128)(2,1)S(1)} %get-tuple-element.26.lbuf, ...), custom_call_target="tpu_custom_call" | custom-call | flops 3000000000 | bytes 1000000 | tf_op jit(solution)/shard_map/sides/pallas_call | solution.py:410
  11.9 2.8 %collective-permute-start.6 = (f32[512,128]{1,0:T(8,128)S(1)}, f32[512,128]{1,0:T(8,128)S(1)}, u32[]{:S(2)}, u32[]{:S(2)}) collective-permute-start(f32[512,128]{1,0:T(8,128)S(1)} %get-tuple-element.38.yea), channel_id=1, source_target_pairs={{0,8},{8,0},{16,24},{24,16},{1,9},{9,1},{17,25},{25,17},{2,10},{10... | collective-permute-start | bytes 786440 | tf_op jit(solution)/shard_map/ppermute | solution.py:314
  14.7 1.8 %collective-permute-start.2 = (f32[1032,128]{1,0:T(8,128)S(1)}, f32[1032,128]{1,0:T(8,128)S(1)}, u32[]{:S(2)}, u32[]{:S(2)}) collective-permute-start(f32[1032,128]{1,0:T(8,128)S(1)} %get-tuple-element.34.after.za), channel_id=1, source_target_pairs={{0,1},{1,0},{2,3},{3,2},{4,5},{5,4},{6,7},{7,6},{8,9},{9,8},{10,11... | collective-permute-start | bytes 1585160 | tf_op jit(solution)/shard_map/ppermute | solution.py:314
  16.5 2.5 %collective-permute-start.3 = (f32[1032,128]{1,0:T(8,128)S(1)}, f32[1032,128]{1,0:T(8,128)S(1)}, u32[]{:S(2)}, u32[]{:S(2)}) collective-permute-start(f32[1032,128]{1,0:T(8,128)S(1)} %get-tuple-element.35.zb), channel_id=1, source_target_pairs={{0,32},{1,2},{2,1},{3,4},{4,3},{5,6},{6,5},{7,39},{32,0},{33,34},{... | collective-permute-start | bytes 1585160 | tf_op jit(solution)/shard_map/ppermute | solution.py:326
  19.0 0.0 collective-permute-start.7
  19.0 0.5 %collective-permute-start.4 = (f32[128,128]{1,0:T(8,128)S(1)}, f32[128,128]{1,0:T(8,128)S(1)}, u32[]{:S(2)}, u32[]{:S(2)}) collective-permute-start(f32[128,128]{1,0:T(8,128)S(1)} %get-tuple-element.36.xa), channel_id=1, source_target_pairs={{0,32},{32,0},{64,96},{96,64},{1,33},{33,1},{65,97},{97,65},{2,34}... | collective-permute-start | bytes 196616 | tf_op jit(solution)/shard_map/ppermute | solution.py:314
  19.5 1.0 %collective-permute-done.6.fyea = f32[512,128]{1,0:T(8,128)S(1)} collective-permute-done((f32[512,128]{1,0:T(8,128)S(1)}, f32[512,128]{1,0:T(8,128)S(1)}, u32[]{:S(2)}, u32[]{:S(2)}) %collective-permute-start.6) | collective-permute-done | bytes 262176 | tf_op jit(solution)/shard_map/ppermute | solution.py:314
  20.5 0.7 %collective-permute-start.5 = (f32[128,128]{1,0:T(8,128)S(1)}, f32[128,128]{1,0:T(8,128)S(1)}, u32[]{:S(2)}, u32[]{:S(2)}) collective-permute-start(f32[128,128]{1,0:T(8,128)S(1)} %get-tuple-element.37.xb), channel_id=1, source_target_pairs={{0,96},{32,64},{64,32},{96,0},{1,97},{33,65},{65,33},{97,1},{2,98}... | collective-permute-start | bytes 196616 | tf_op jit(solution)/shard_map/ppermute | solution.py:320
  21.2 3.5 %rest.1.before = f32[1536,1536]{1,0:T(8,128)} custom-call(s32[8,128]{1,0:T(8,128)S(1)} %get-tuple-element.24.spots, bf16[9216,128]{1,0:T(8,128)(2,1)S(1)} %get-tuple-element.25.sall, bf16[1536,512]{1,0:T(8,128)(2,1)S(1)} %get-tuple-element.28.wbd, bf16[1536,512]{1,0:T(8,128)(2,1)S(1)} %get-tuple-element.40.wac, bf16[1536,512]{1,0:T(8,128)(2,1)S(1)} %get-tuple-element.41.wef, ...), custom_call_target="tpu_custom_call" | custom-call | flops 3000000000 | bytes 8000000 | tf_op jit(solution)/shard_map/rest/pallas_call | solution.py:430
  24.7 0.0 collective-permute-done.7.fyeb
  24.8 1.0 %borders.1.before = f32[1536,1536]{1,0:T(8,128)} custom-call(s32[8,128]{1,0:T(8,128)S(1)} %get-tuple-element.24.spots, f32[512,128]{1,0:T(8,128)S(1)} %get-tuple-element.38.yea, f32[512,128]{1,0:T(8,128)S(1)} %get-tuple-element.39.yeb, f32[512,128]{1,0:T(8,128)S(1)} %collective-permute-done.6.fyea, ...), custom_call_target="tpu_custom_call", output_to_operand_aliasing={{}: (5, {})} | custom-call | flops 100000000 | bytes 1000000 | tf_op jit(solution)/shard_map/borders/pallas_call | solution.py:444
  25.8 0.0 collective-permute-done.4.fxa
  25.8 5.0 %collective-permute-done.5.fxb = f32[128,128]{1,0:T(8,128)S(1)} collective-permute-done((f32[128,128]{1,0:T(8,128)S(1)}, f32[128,128]{1,0:T(8,128)S(1)}, u32[]{:S(2)}, u32[]{:S(2)}) %collective-permute-start.5) | collective-permute-done | bytes 65568 | tf_op jit(solution)/shard_map/ppermute | solution.py:320
  30.8 0.0 collective-permute-done.2.fza
  30.8 2.6 %collective-permute-done.3.fzb = f32[1032,128]{1,0:T(8,128)S(1)} collective-permute-done((f32[1032,128]{1,0:T(8,128)S(1)}, f32[1032,128]{1,0:T(8,128)S(1)}, u32[]{:S(2)}, u32[]{:S(2)}) %collective-permute-start.3) | collective-permute-done | bytes 528416 | tf_op jit(solution)/shard_map/ppermute | solution.py:326
  33.5 1.5 %last.1 = f32[1536,1536]{1,0:T(8,128)} custom-call(s32[8,128]{1,0:T(8,128)S(1)} %get-tuple-element.24.spots, f32[1032,128]{1,0:T(8,128)S(1)} %get-tuple-element.34.after.za, f32[1032,128]{1,0:T(8,128)S(1)} %get-tuple-element.35.zb, f32[1032,128]{1,0:T(8,128)S(1)} %collective-permute-done.2.fza, ...), custom_call_target="tpu_custom_call", output_to_operand_aliasing={{}: (9, {})} | custom-call | flops 100000000 | bytes 2000000 | tf_op jit(solution)/shard_map/last/pallas_call | solution.py:455
  (1 shorter events, 0.0 us)
Async XLA Ops:
  4.8 4.4 %collective-permute-start = (f32[136,128]{1,0:T(8,128)S(1)}, f32[136,128]{1,0:T(8,128)S(1)}, u32[]{:S(2)}, u32[]{:S(2)}) collective-permute-start(f32[136,128]{1,0:T(8,128)S(1)} %get-tuple-element.32), channel_id=1, source_target_pairs={{0,8},{8,0},{16,24},{24,16},{1,9},{9,1},{17,25},{25,17},{2,10},{10... | collective-permute-start | bytes 208904 | tf_op jit(solution)/shard_map/ppermute | solution.py:314
  6.5 2.7 %collective-permute-start.1 = (f32[136,128]{1,0:T(8,128)S(1)}, f32[136,128]{1,0:T(8,128)S(1)}, u32[]{:S(2)}, u32[]{:S(2)}) collective-permute-start(f32[136,128]{1,0:T(8,128)S(1)} %get-tuple-element.33), channel_id=1, source_target_pairs={{0,32},{8,16},{16,8},{24,56},{32,0},{40,48},{48,40},{56,24},{64,96... | collective-permute-start | bytes 208904 | tf_op jit(solution)/shard_map/ppermute | solution.py:326
  11.9 8.6 %collective-permute-start.6 = (f32[512,128]{1,0:T(8,128)S(1)}, f32[512,128]{1,0:T(8,128)S(1)}, u32[]{:S(2)}, u32[]{:S(2)}) collective-permute-start(f32[512,128]{1,0:T(8,128)S(1)} %get-tuple-element.38.yea), channel_id=1, source_target_pairs={{0,8},{8,0},{16,24},{24,16},{1,9},{9,1},{17,25},{25,17},{2,10},{10... | collective-permute-start | bytes 786440 | tf_op jit(solution)/shard_map/ppermute | solution.py:314
  14.7 16.2 %collective-permute-start.2 = (f32[1032,128]{1,0:T(8,128)S(1)}, f32[1032,128]{1,0:T(8,128)S(1)}, u32[]{:S(2)}, u32[]{:S(2)}) collective-permute-start(f32[1032,128]{1,0:T(8,128)S(1)} %get-tuple-element.34.after.za), channel_id=1, source_target_pairs={{0,1},{1,0},{2,3},{3,2},{4,5},{5,4},{6,7},{7,6},{8,9},{9,8},{10,11... | collective-permute-start | bytes 1585160 | tf_op jit(solution)/shard_map/ppermute | solution.py:314
  16.5 16.9 %collective-permute-start.3 = (f32[1032,128]{1,0:T(8,128)S(1)}, f32[1032,128]{1,0:T(8,128)S(1)}, u32[]{:S(2)}, u32[]{:S(2)}) collective-permute-start(f32[1032,128]{1,0:T(8,128)S(1)} %get-tuple-element.35.zb), channel_id=1, source_target_pairs={{0,32},{1,2},{2,1},{3,4},{4,3},{5,6},{6,5},{7,39},{32,0},{33,34},{... | collective-permute-start | bytes 1585160 | tf_op jit(solution)/shard_map/ppermute | solution.py:326
  19.0 5.8 %collective-permute-start.7 = (f32[512,128]{1,0:T(8,128)S(1)}, f32[512,128]{1,0:T(8,128)S(1)}, u32[]{:S(2)}, u32[]{:S(2)}) collective-permute-start(f32[512,128]{1,0:T(8,128)S(1)} %get-tuple-element.39.yeb), channel_id=1, source_target_pairs={{0,32},{8,16},{16,8},{24,56},{32,0},{40,48},{48,40},{56,24},{64,96... | collective-permute-start | bytes 786440 | tf_op jit(solution)/shard_map/ppermute | solution.py:326
  19.0 6.8 %collective-permute-start.4 = (f32[128,128]{1,0:T(8,128)S(1)}, f32[128,128]{1,0:T(8,128)S(1)}, u32[]{:S(2)}, u32[]{:S(2)}) collective-permute-start(f32[128,128]{1,0:T(8,128)S(1)} %get-tuple-element.36.xa), channel_id=1, source_target_pairs={{0,32},{32,0},{64,96},{96,64},{1,33},{33,1},{65,97},{97,65},{2,34}... | collective-permute-start | bytes 196616 | tf_op jit(solution)/shard_map/ppermute | solution.py:314
  20.5 10.4 %collective-permute-start.5 = (f32[128,128]{1,0:T(8,128)S(1)}, f32[128,128]{1,0:T(8,128)S(1)}, u32[]{:S(2)}, u32[]{:S(2)}) collective-permute-start(f32[128,128]{1,0:T(8,128)S(1)} %get-tuple-element.37.xb), channel_id=1, source_target_pairs={{0,96},{32,64},{64,32},{96,0},{1,97},{33,65},{65,33},{97,1},{2,98}... | collective-permute-start | bytes 196616 | tf_op jit(solution)/shard_map/ppermute | solution.py:320
where the time goes:
time: 35.1 us; the launch traced here: 34.9 us
  Pallas kernels  16 us (46%)
  starting transfers between devices  9.98 us (28%)
  waiting for transfers between devices  8.9 us (25%)
    ppermute x4, starting transfers between devices, exchange_high(): lax.ppermute(value, axis, [(i, i ^ 1) for i in range(lax.axis_size(axis))])  6.77 us
    ppermute x1, waiting for transfers between devices, exchange_low(): return lax.ppermute(value, axis, [(i, size - 1 - i) for i in range(size)])  5.03 us
    pallas_call x1, Pallas kernels, shards(): pl.pallas_call(edge_kernel, out_shape=(shape(rows, rows, dtype=half), sha...  4.8 us
    pallas_call x1, Pallas kernels, shards(): pl.pallas_call(rest_kernel, out_shape=shape(size, size), in_specs=[VMEM]...  3.52 us
    pallas_call x1, Pallas kernels, shards(): pl.pallas_call(side_kernel, out_shape=(shape(rows, 512, dtype=half), shap...  2.67 us
    ppermute x3, waiting for transfers between devices, exchange_low(): return lax.ppermute(value, ('gx', axis), pairs)  2.64 us
    ppermute x3, starting transfers between devices, exchange_low(): return lax.ppermute(value, ('gx', axis), pairs)  2.47 us
    pallas_call x1, Pallas kernels, shards(): pl.pallas_call(face_kernel, out_shape=(shape(rows, 512, dtype=half), shap...  2.46 us
  transfers between devices with their start and end apart: 8, of which 4 were waited for; matrix products, arithmetic and copies ran while one was open for 0% of the time, Pallas kernels for 20%

commit v1 on v0

--- a/solution.py
+++ b/solution.py
@@ -281,17 +281,18 @@
     writer.finish()
 
 
-def border_kernel(spots, yea, yeb, fyea, fyeb, before, out, stage, wsem):
+def border_kernel(spots, yea, yeb, fyea, fyeb, xa, fxa, before, out, stage, wsem):
     del before
     writer = Writer(spots, out, stage, wsem)
     for n, (k, l) in enumerate(Y_HIGH):
         writer.emit(k, l, yea[slot(n)] + fyea[slot(n)])
     for n, (k, l) in enumerate(Y_LOW):
         writer.emit(k, l, yeb[slot(n)] + known("gy", fyeb[slot(n)]))
+    writer.emit(1, 1, xa[...] + fxa[...])
     writer.finish()
 
 
-def last_kernel(spots, za, zb, fza, fzb, xa, xb, fxa, fxb, before, out, stage, wsem):
+def last_kernel(spots, za, zb, fza, fzb, before, out, stage, wsem):
     del before
     writer = Writer(spots, out, stage, wsem)
     for pairs, packs, own, other, take in (
@@ -305,8 +306,13 @@
             first, second = unpack(own[slot(6 + n)] + take(other[slot(6 + n)]), own[row] + take(other[row]))
             writer.emit(k, k, first)
             writer.emit(l, l, second)
+    writer.finish()
+
+
+def corner_kernel(spots, xb, fxb, before, out, stage, wsem):
+    del before
+    writer = Writer(spots, out, stage, wsem)
     writer.emit(0, 0, xb[...] + known("gx", fxb[...]))
-    writer.emit(1, 1, xa[...] + fxa[...])
     writer.finish()
 
 
@@ -317,7 +323,13 @@
 def exchange_low(value, axis):
     size, across = lax.axis_size(axis), lax.axis_size("gx")
     if axis == "gx":
-        return lax.ppermute(value, axis, [(i, size - 1 - i) for i in range(size)])
+        rows = lax.axis_size("gy")
+        pairs = []
+        for i in range(size):
+            for y in range(rows):
+                to = (i, y ^ 1) if i in (0, size - 1) else (size - 1 - i, y)
+                pairs.append((i * rows + y, to[0] * rows + to[1]))
+        return lax.ppermute(value, ("gx", "gy"), pairs)
     pairs = []
     for x in range(across):
         for i in range(size):
@@ -444,25 +456,36 @@
     out = pl.pallas_call(
         border_kernel,
         out_shape=shape(size, size),
-        in_specs=[VMEM] * 5 + [HBM],
+        in_specs=[VMEM] * 7 + [HBM],
         out_specs=HBM,
-        scratch_shapes=[pltpu.VMEM((14 * BLK, BLK), jnp.float32), DMA],
-        input_output_aliases={5: 0},
+        scratch_shapes=[pltpu.VMEM((15 * BLK, BLK), jnp.float32), DMA],
+        input_output_aliases={7: 0},
         compiler_params=params(4),
         cost_estimate=cost(0.1, 1),
         name="borders",
-    )(spots, yea, yeb, fyea, fyeb, out)
+    )(spots, yea, yeb, fyea, fyeb, xa, fxa, out)
     out = pl.pallas_call(
         last_kernel,
         out_shape=shape(size, size),
-        in_specs=[VMEM] * 9 + [HBM],
+        in_specs=[VMEM] * 5 + [HBM],
         out_specs=HBM,
-        scratch_shapes=[pltpu.VMEM((34 * BLK, BLK), jnp.float32), DMA],
-        input_output_aliases={9: 0},
+        scratch_shapes=[pltpu.VMEM((32 * BLK, BLK), jnp.float32), DMA],
+        input_output_aliases={5: 0},
         compiler_params=params(8),
         cost_estimate=cost(0.1, 2),
         name="last",
-    )(spots, za, zb, fza, fzb, xa, xb, fxa, fxb, out)
+    )(spots, za, zb, fza, fzb, out)
+    out = pl.pallas_call(
+        corner_kernel,
+        out_shape=shape(size, size),
+        in_specs=[VMEM] * 3 + [HBM],
+        out_specs=HBM,
+        scratch_shapes=[pltpu.VMEM((BLK, BLK), jnp.float32), DMA],
+        input_output_aliases={3: 0},
+        compiler_params=params(2),
+        cost_estimate=cost(0.01, 0.1),
+        name="end",
+    )(spots, xb, fxb, out)
     return out.reshape(1, 1, 1, size, size)
 
 

time: 35.1 us -> 31.8 us (0.906)
  the two profiles are of different devices: /device:TPU:4 before, /device:TPU:12 now
where the time goes in v1:
time: 31.8 us; the launch traced here: 31.6 us
  Pallas kernels  16.6 us (52%)
  starting transfers between devices  9.72 us (31%)
  waiting for transfers between devices  5.15 us (16%)
    ppermute x3, starting transfers between devices, exchange_low(): return lax.ppermute(value, ('gx', axis), pairs)  6.85 us
    pallas_call x1, Pallas kernels, shards(): pl.pallas_call(edge_kernel, out_shape=(shape(rows, rows, dtype=half), sha...  4.8 us
    pallas_call x1, Pallas kernels, shards(): pl.pallas_call(rest_kernel, out_shape=shape(size, size), in_specs=[VMEM]...  3.53 us
    ppermute x4, waiting for transfers between devices, exchange_high(): lax.ppermute(value, axis, [(i, i ^ 1) for i in range(lax.axis_size(axis))])  2.93 us
    pallas_call x1, Pallas kernels, shards(): pl.pallas_call(side_kernel, out_shape=(shape(rows, 512, dtype=half), shap...  2.67 us
    ppermute x4, starting transfers between devices, exchange_high(): lax.ppermute(value, axis, [(i, i ^ 1) for i in range(lax.axis_size(axis))])  2.63 us
    pallas_call x1, Pallas kernels, shards(): pl.pallas_call(face_kernel, out_shape=(shape(rows, 512, dtype=half), shap...  2.46 us
    ppermute x3, waiting for transfers between devices, exchange_low(): return lax.ppermute(value, ('gx', axis), pairs)  2.21 us
  transfers between devices with their start and end apart: 8, of which 3 were waited for; matrix products, arithmetic and copies ran while one was open for 0% of the time, Pallas kernels for 35%

profile of v1, /device:TPU:12, one launch (start us, length us, event | category | flops | bytes accessed | tf_op | source)
XLA Modules:
  0.0 31.6 jit_solution(5316170193285628687)
XLA Ops:
  0.0 4.8 %edges.1 = (bf16[1536,1536]{1,0:T(8,128)(2,1)S(1)}, bf16[1536,1536]{1,0:T(8,128)(2,1)S(1)}, bf16[9216,128]{1,0:T(8,128)(2,1)S(1)}, bf16[1536,512]{1,0:T(8,128)(2...) custom-call(s32[12]{0:T(128)} %bitcast.8, ...), custom_call_target="tpu_custom_call" | custom-call | flops 3000000000 | bytes 8000000 | tf_op jit(solution)/shard_map/edges/pallas_call | solution.py:380
  4.8 0.5 %collective-permute-start = (f32[136,128]{1,0:T(8,128)S(1)}, f32[136,128]{1,0:T(8,128)S(1)}, u32[]{:S(2)}, u32[]{:S(2)}) collective-permute-start(f32[136,128]{1,0:T(8,128)S(1)} %get-tuple-element.32), channel_id=1, source_target_pairs={{0,8},{8,0},{16,24},{24,16},{1,9},{9,1},{17,25},{25,17},{2,10},{10... | collective-permute-start | bytes 208904 | tf_op jit(solution)/shard_map/ppermute | solution.py:320
  5.3 2.5 %collective-permute-start.1 = (f32[136,128]{1,0:T(8,128)S(1)}, f32[136,128]{1,0:T(8,128)S(1)}, u32[]{:S(2)}, u32[]{:S(2)}) collective-permute-start(f32[136,128]{1,0:T(8,128)S(1)} %get-tuple-element.33), channel_id=1, source_target_pairs={{0,32},{8,16},{16,8},{24,56},{32,0},{40,48},{48,40},{56,24},{64,96... | collective-permute-start | bytes 208904 | tf_op jit(solution)/shard_map/ppermute | solution.py:338
  7.8 2.5 %faces.1 = (bf16[1536,512]{1,0:T(8,128)(2,1)S(1)}, f32[1032,128]{1,0:T(8,128)S(1)}, f32[1032,128]{1,0:T(8,128)S(1)}) custom-call(bf16[9216,128]{1,0:T(8,128)(2,1)S(1)} %get-tuple-element.25.sall, bf16[1536,1536]{1,0:T(8,128)(2,1)S(1)} %get-tuple-element.26.lbuf, bf16[1536,1536]{1,0:T(8,128)(2,1)S(1)} %get-tuple-element.27.cbuf, ...), custom_call_target="tpu_custom_call" | custom-call | flops 3000000000 | bytes 1000000 | tf_op jit(solution)/shard_map/faces/pallas_call | solution.py:401
  10.3 0.0 collective-permute-done.fya
  10.3 0.0 collective-permute-done.1.fyb
  10.3 1.9 %collective-permute-start.3 = (f32[1032,128]{1,0:T(8,128)S(1)}, f32[1032,128]{1,0:T(8,128)S(1)}, u32[]{:S(2)}, u32[]{:S(2)}) collective-permute-start(f32[1032,128]{1,0:T(8,128)S(1)} %get-tuple-element.34.after.za), channel_id=1, source_target_pairs={{0,1},{1,0},{2,3},{3,2},{4,5},{5,4},{6,7},{7,6},{8,9},{9,8},{10,11... | collective-permute-start | bytes 1585160 | tf_op jit(solution)/shard_map/ppermute | solution.py:320
  12.3 2.5 %collective-permute-start.4 = (f32[1032,128]{1,0:T(8,128)S(1)}, f32[1032,128]{1,0:T(8,128)S(1)}, u32[]{:S(2)}, u32[]{:S(2)}) collective-permute-start(f32[1032,128]{1,0:T(8,128)S(1)} %get-tuple-element.36.zb), channel_id=1, source_target_pairs={{0,32},{1,2},{2,1},{3,4},{4,3},{5,6},{6,5},{7,39},{32,0},{33,34},{... | collective-permute-start | bytes 1585160 | tf_op jit(solution)/shard_map/ppermute | solution.py:338
  14.7 2.7 %sides.1 = (bf16[1536,512]{1,0:T(8,128)(2,1)S(1)}, f32[512,128]{1,0:T(8,128)S(1)}, f32[512,128]{1,0:T(8,128)S(1)}, f32[128,128]{1,0:T(8,128)S(1)}, f32[128,128]{1,0:T(8,128)S(1)}, /*index=5*/f32[1024,128]{1,0:T(8,128)S(1)}) custom-call(bf16[9216,128]{1,0:T(8,128)(2,1)S(1)} %get-tuple-element.25.sall, bf16[1536,1536]{1,0:T(8,128)(2,1)S(1)} %get-tuple-element.26.lbuf, ...), custom_call_target="tpu_custom_call" | custom-call | flops 3000000000 | bytes 1000000 | tf_op jit(solution)/shard_map/sides/pallas_call | solution.py:422
  17.4 0.1 collective-permute-start.7
  17.5 0.1 collective-permute-start.5
  17.6 1.9 %collective-permute-start.6 = (f32[512,128]{1,0:T(8,128)S(1)}, f32[512,128]{1,0:T(8,128)S(1)}, u32[]{:S(2)}, u32[]{:S(2)}) collective-permute-start(f32[512,128]{1,0:T(8,128)S(1)} %get-tuple-element.38.yeb), channel_id=1, source_target_pairs={{0,32},{8,16},{16,8},{24,56},{32,0},{40,48},{48,40},{56,24},{64,96... | collective-permute-start | bytes 786440 | tf_op jit(solution)/shard_map/ppermute | solution.py:338
  19.5 0.0 collective-permute-done.7.fxa
  19.5 0.3 collective-permute-start.2
  19.8 3.5 %rest.1.before = f32[1536,1536]{1,0:T(8,128)} custom-call(s32[8,128]{1,0:T(8,128)S(1)} %get-tuple-element.24.spots, bf16[9216,128]{1,0:T(8,128)(2,1)S(1)} %get-tuple-element.25.sall, bf16[1536,512]{1,0:T(8,128)(2,1)S(1)} %get-tuple-element.28.wbd, bf16[1536,512]{1,0:T(8,128)(2,1)S(1)} %get-tuple-element.40.wac, bf16[1536,512]{1,0:T(8,128)(2,1)S(1)} %get-tuple-element.41.wef, ...), custom_call_target="tpu_custom_call" | custom-call | flops 3000000000 | bytes 8000000 | tf_op jit(solution)/shard_map/rest/pallas_call | solution.py:442
  23.3 2.9 %collective-permute-done.5.fyea = f32[512,128]{1,0:T(8,128)S(1)} collective-permute-done((f32[512,128]{1,0:T(8,128)S(1)}, f32[512,128]{1,0:T(8,128)S(1)}, u32[]{:S(2)}, u32[]{:S(2)}) %collective-permute-start.5) | collective-permute-done | bytes 262176 | tf_op jit(solution)/shard_map/ppermute | solution.py:320
  26.2 0.1 collective-permute-done.6.fyeb
  26.3 1.1 %borders.1.before = f32[1536,1536]{1,0:T(8,128)} custom-call(s32[8,128]{1,0:T(8,128)S(1)} %get-tuple-element.24.spots, f32[512,128]{1,0:T(8,128)S(1)} %get-tuple-element.37.yea, f32[512,128]{1,0:T(8,128)S(1)} %get-tuple-element.38.yeb, f32[512,128]{1,0:T(8,128)S(1)} %collective-permute-done.5.fyea, ...), custom_call_target="tpu_custom_call", output_to_operand_aliasing={{}: (7, {})} | custom-call | flops 100000000 | bytes 1000000 | tf_op jit(solution)/shard_map/borders/pallas_call | solution.py:456
  27.4 0.0 collective-permute-done.3.fza
  27.4 2.1 %collective-permute-done.4.fzb = f32[1032,128]{1,0:T(8,128)S(1)} collective-permute-done((f32[1032,128]{1,0:T(8,128)S(1)}, f32[1032,128]{1,0:T(8,128)S(1)}, u32[]{:S(2)}, u32[]{:S(2)}) %collective-permute-start.4) | collective-permute-done | bytes 528416 | tf_op jit(solution)/shard_map/ppermute | solution.py:338
  29.5 1.4 %last.1.before = f32[1536,1536]{1,0:T(8,128)} custom-call(s32[8,128]{1,0:T(8,128)S(1)} %get-tuple-element.24.spots, f32[1032,128]{1,0:T(8,128)S(1)} %get-tuple-element.34.after.za, f32[1032,128]{1,0:T(8,128)S(1)} %get-tuple-element.36.zb, f32[1032,128]{1,0:T(8,128)S(1)} %collective-permute-done.3.fza, ...), custom_call_target="tpu_custom_call", output_to_operand_aliasing={{}: (5, {})} | custom-call | flops 100000000 | bytes 2000000 | tf_op jit(solution)/shard_map/last/pallas_call | solution.py:467
  30.9 0.0 collective-permute-done.2.fxb
  30.9 0.7 %end.1 = f32[1536,1536]{1,0:T(8,128)} custom-call(s32[8,128]{1,0:T(8,128)S(1)} %get-tuple-element.24.spots, f32[128,128]{1,0:T(8,128)S(1)} %get-tuple-element.35.xb, f32[128,128]{1,0:T(8,128)S(1)} %collective-permute-done.2.fxb, f32[1536,1536]{1,0:T(8,128)} %last.1.before), custom_call_target="tpu_custom_call", output_to_operand_aliasing={{}: (3, {})} | custom-call | flops 10000000 | bytes 100000 | tf_op jit(solution)/shard_map/end/pallas_call | solution.py:478
  (1 shorter events, 0.0 us)
Async XLA Ops:
  4.8 5.5 %collective-permute-start = (f32[136,128]{1,0:T(8,128)S(1)}, f32[136,128]{1,0:T(8,128)S(1)}, u32[]{:S(2)}, u32[]{:S(2)}) collective-permute-start(f32[136,128]{1,0:T(8,128)S(1)} %get-tuple-element.32), channel_id=1, source_target_pairs={{0,8},{8,0},{16,24},{24,16},{1,9},{9,1},{17,25},{25,17},{2,10},{10... | collective-permute-start | bytes 208904 | tf_op jit(solution)/shard_map/ppermute | solution.py:320
  5.3 5.0 %collective-permute-start.1 = (f32[136,128]{1,0:T(8,128)S(1)}, f32[136,128]{1,0:T(8,128)S(1)}, u32[]{:S(2)}, u32[]{:S(2)}) collective-permute-start(f32[136,128]{1,0:T(8,128)S(1)} %get-tuple-element.33), channel_id=1, source_target_pairs={{0,32},{8,16},{16,8},{24,56},{32,0},{40,48},{48,40},{56,24},{64,96... | collective-permute-start | bytes 208904 | tf_op jit(solution)/shard_map/ppermute | solution.py:338
  10.3 17.0 %collective-permute-start.3 = (f32[1032,128]{1,0:T(8,128)S(1)}, f32[1032,128]{1,0:T(8,128)S(1)}, u32[]{:S(2)}, u32[]{:S(2)}) collective-permute-start(f32[1032,128]{1,0:T(8,128)S(1)} %get-tuple-element.34.after.za), channel_id=1, source_target_pairs={{0,1},{1,0},{2,3},{3,2},{4,5},{5,4},{6,7},{7,6},{8,9},{9,8},{10,11... | collective-permute-start | bytes 1585160 | tf_op jit(solution)/shard_map/ppermute | solution.py:320
  12.3 17.2 %collective-permute-start.4 = (f32[1032,128]{1,0:T(8,128)S(1)}, f32[1032,128]{1,0:T(8,128)S(1)}, u32[]{:S(2)}, u32[]{:S(2)}) collective-permute-start(f32[1032,128]{1,0:T(8,128)S(1)} %get-tuple-element.36.zb), channel_id=1, source_target_pairs={{0,32},{1,2},{2,1},{3,4},{4,3},{5,6},{6,5},{7,39},{32,0},{33,34},{... | collective-permute-start | bytes 1585160 | tf_op jit(solution)/shard_map/ppermute | solution.py:338
  17.4 2.1 %collective-permute-start.7 = (f32[128,128]{1,0:T(8,128)S(1)}, f32[128,128]{1,0:T(8,128)S(1)}, u32[]{:S(2)}, u32[]{:S(2)}) collective-permute-start(f32[128,128]{1,0:T(8,128)S(1)} %get-tuple-element.39.xa), channel_id=1, source_target_pairs={{0,32},{32,0},{64,96},{96,64},{1,33},{33,1},{65,97},{97,65},{2,34}... | collective-permute-start | bytes 196616 | tf_op jit(solution)/shard_map/ppermute | solution.py:320
  17.5 8.7 %collective-permute-start.5 = (f32[512,128]{1,0:T(8,128)S(1)}, f32[512,128]{1,0:T(8,128)S(1)}, u32[]{:S(2)}, u32[]{:S(2)}) collective-permute-start(f32[512,128]{1,0:T(8,128)S(1)} %get-tuple-element.37.yea), channel_id=1, source_target_pairs={{0,8},{8,0},{16,24},{24,16},{1,9},{9,1},{17,25},{25,17},{2,10},{10... | collective-permute-start | bytes 786440 | tf_op jit(solution)/shard_map/ppermute | solution.py:320
  17.6 8.7 %collective-permute-start.6 = (f32[512,128]{1,0:T(8,128)S(1)}, f32[512,128]{1,0:T(8,128)S(1)}, u32[]{:S(2)}, u32[]{:S(2)}) collective-permute-start(f32[512,128]{1,0:T(8,128)S(1)} %get-tuple-element.38.yeb), channel_id=1, source_target_pairs={{0,32},{8,16},{16,8},{24,56},{32,0},{40,48},{48,40},{56,24},{64,96... | collective-permute-start | bytes 786440 | tf_op jit(solution)/shard_map/ppermute | solution.py:338
  19.5 11.4 %collective-permute-start.2 = (f32[128,128]{1,0:T(8,128)S(1)}, f32[128,128]{1,0:T(8,128)S(1)}, u32[]{:S(2)}, u32[]{:S(2)}) collective-permute-start(f32[128,128]{1,0:T(8,128)S(1)} %get-tuple-element.35.xb), channel_id=1, source_target_pairs={{0,8},{8,0},{16,24},{24,16},{32,64},{40,72},{48,80},{56,88},{64,32... | collective-permute-start | bytes 196616 | tf_op jit(solution)/shard_map/ppermute | solution.py:332

commit v2 on v1

--- a/solution.py
+++ b/solution.py
@@ -17,7 +17,8 @@
 Y_HIGH, Y_LOW = ((3, 3), (3, 9), (3, 11), (9, 11)), ((2, 2), (2, 8), (2, 10), (8, 10))
 KEPT = ((2, 3), (2, 9), (3, 8), (2, 11), (3, 10), (8, 11), (9, 10), (0, 1))
 FACES = 8 * BLK
-GROUPS = ((0, 2), (2, 4), (4, 6))
+GROUPS = ((0, 1), (1, 3), (3, 6))
+HEAD = GROUPS[0][1] * PAN
 MESSAGE = FACES + 8
 
 
@@ -108,7 +109,7 @@
 EDGE_BLOCKS = ((8, 8), (8, 9), (9, 9), (10, 10), (10, 11), (11, 11))
 
 
-def edge_kernel(order, inverse, coupling, stiff, lbuf, cbuf, sall, wbd, yda, ydb, zpart, spots, osmem, sbuf, osem, lsem, csem, rsem, ssem):
+def edge_kernel(order, inverse, coupling, stiff, lbuf, cbuf, sall, wbd, yda, ydb, zpart, spots, osmem, sbuf, crow, osem, hsem, lsem, csem, rsem, ssem):
     fetch = fetch_order(order, osmem, osem)
     panels = lbuf.shape[0] // PAN
     lcopies = [
@@ -119,14 +120,15 @@
         )
         for pan in range(panels)
     ]
-    for copy in lcopies:
+    head = pltpu.make_async_copy(coupling.at[pl.ds(0, HEAD), :], crow, hsem)
+    for copy in (*lcopies[: GROUPS[0][1]], head, *lcopies[GROUPS[0][1] :]):
         copy.start()
     fetch.wait()
     at = positions(osmem)
     lane = lax.broadcasted_iota(jnp.int32, (8, BLK), 1)
     spots[...] = sum(jnp.where(lane == k, at[k], 0) for k in range(NBLK))
     ccopies = []
-    for lo, hi in GROUPS:
+    for lo, hi in GROUPS[1:]:
         rows = pl.ds(lo * PAN, (hi - lo) * PAN)
         group = [
             pltpu.make_async_copy(
@@ -147,11 +149,14 @@
         for n, k in enumerate(COLUMNS[4:])
     ]
     later += stiff_copies(at, stiff, sall, rsem, LATER)
-    for (lo, hi), group in zip(GROUPS, ccopies):
+    for (lo, hi), group in zip(GROUPS, [[head], *ccopies]):
         for pan in range(lo, hi):
             lcopies[pan].wait()
         for copy in group:
             copy.wait()
+        if lo == 0:
+            for n, k in enumerate(COLUMNS[:4]):
+                cbuf[:HEAD, slot(n)] = crow[:, pl.ds(at[k], BLK)]
         if lo == 0:
             for copy in later:
                 copy.start()
@@ -391,7 +396,7 @@
         ),
         in_specs=[HBM] * 4,
         out_specs=(VMEM,) * 8,
-        scratch_shapes=[osmem, pltpu.VMEM((len(EDGE_BLOCKS) * BLK, BLK), half), DMA, DMA((panels,)), DMA((panels,)), DMA, DMA],
+        scratch_shapes=[osmem, pltpu.VMEM((len(EDGE_BLOCKS) * BLK, BLK), half), pltpu.VMEM((HEAD, size), half), DMA, DMA, DMA((panels,)), DMA((panels,)), DMA, DMA],
         compiler_params=params(12),
         cost_estimate=cost(3, 8),
         name="edges",

time: 31.8 us -> 31.7 us (level)
  no operation moved by 1% of the time
where the time goes in v2:
time: 31.7 us; the launch traced here: 31.6 us
  Pallas kernels  16.6 us (52%)
  starting transfers between devices  9.72 us (31%)
  waiting for transfers between devices  5.15 us (16%)
    ppermute x3, starting transfers between devices, exchange_low(): return lax.ppermute(value, ('gx', axis), pairs)  6.77 us
    pallas_call x1, Pallas kernels, shards(): pl.pallas_call(edge_kernel, out_shape=(shape(rows, rows, dtype=half), sha...  4.79 us
    pallas_call x1, Pallas kernels, shards(): pl.pallas_call(rest_kernel, out_shape=shape(size, size), in_specs=[VMEM]...  3.53 us
    ppermute x4, waiting for transfers between devices, exchange_high(): lax.ppermute(value, axis, [(i, i ^ 1) for i in range(lax.axis_size(axis))])  2.93 us
    ppermute x4, starting transfers between devices, exchange_high(): lax.ppermute(value, axis, [(i, i ^ 1) for i in range(lax.axis_size(axis))])  2.69 us
    pallas_call x1, Pallas kernels, shards(): pl.pallas_call(side_kernel, out_shape=(shape(rows, 512, dtype=half), shap...  2.67 us
    pallas_call x1, Pallas kernels, shards(): pl.pallas_call(face_kernel, out_shape=(shape(rows, 512, dtype=half), shap...  2.46 us
    ppermute x3, waiting for transfers between devices, exchange_low(): return lax.ppermute(value, ('gx', axis), pairs)  2.21 us
  transfers between devices with their start and end apart: 8, of which 3 were waited for; matrix products, arithmetic and copies ran while one was open for 0% of the time, Pallas kernels for 35%

profile of v2, /device:TPU:12, one launch (start us, length us, event | category | flops | bytes accessed | tf_op | source)
XLA Modules:
  0.0 31.6 jit_solution(4520062165266120377)
XLA Ops:
  0.0 4.8 %edges.1 = (bf16[1536,1536]{1,0:T(8,128)(2,1)S(1)}, bf16[1536,1536]{1,0:T(8,128)(2,1)S(1)}, bf16[9216,128]{1,0:T(8,128)(2,1)S(1)}, bf16[1536,512]{1,0:T(8,128)(2...) custom-call(s32[12]{0:T(128)} %bitcast.8, ...), custom_call_target="tpu_custom_call" | custom-call | flops 3000000000 | bytes 8000000 | tf_op jit(solution)/shard_map/edges/pallas_call | solution.py:385
  4.8 0.5 %collective-permute-start = (f32[136,128]{1,0:T(8,128)S(1)}, f32[136,128]{1,0:T(8,128)S(1)}, u32[]{:S(2)}, u32[]{:S(2)}) collective-permute-start(f32[136,128]{1,0:T(8,128)S(1)} %get-tuple-element.32), channel_id=1, source_target_pairs={{0,8},{8,0},{16,24},{24,16},{1,9},{9,1},{17,25},{25,17},{2,10},{10... | collective-permute-start | bytes 208904 | tf_op jit(solution)/shard_map/ppermute | solution.py:325
  5.3 2.4 %collective-permute-start.1 = (f32[136,128]{1,0:T(8,128)S(1)}, f32[136,128]{1,0:T(8,128)S(1)}, u32[]{:S(2)}, u32[]{:S(2)}) collective-permute-start(f32[136,128]{1,0:T(8,128)S(1)} %get-tuple-element.33), channel_id=1, source_target_pairs={{0,32},{8,16},{16,8},{24,56},{32,0},{40,48},{48,40},{56,24},{64,96... | collective-permute-start | bytes 208904 | tf_op jit(solution)/shard_map/ppermute | solution.py:343
  7.7 2.5 %faces.1 = (bf16[1536,512]{1,0:T(8,128)(2,1)S(1)}, f32[1032,128]{1,0:T(8,128)S(1)}, f32[1032,128]{1,0:T(8,128)S(1)}) custom-call(bf16[9216,128]{1,0:T(8,128)(2,1)S(1)} %get-tuple-element.25.sall, bf16[1536,1536]{1,0:T(8,128)(2,1)S(1)} %get-tuple-element.26.lbuf, bf16[1536,1536]{1,0:T(8,128)(2,1)S(1)} %get-tuple-element.27.cbuf, ...), custom_call_target="tpu_custom_call" | custom-call | flops 3000000000 | bytes 1000000 | tf_op jit(solution)/shard_map/faces/pallas_call | solution.py:406
  10.2 0.0 collective-permute-done.fya
  10.2 0.0 collective-permute-done.1.fyb
  10.3 2.0 %collective-permute-start.3 = (f32[1032,128]{1,0:T(8,128)S(1)}, f32[1032,128]{1,0:T(8,128)S(1)}, u32[]{:S(2)}, u32[]{:S(2)}) collective-permute-start(f32[1032,128]{1,0:T(8,128)S(1)} %get-tuple-element.34.after.za), channel_id=1, source_target_pairs={{0,1},{1,0},{2,3},{3,2},{4,5},{5,4},{6,7},{7,6},{8,9},{9,8},{10,11... | collective-permute-start | bytes 1585160 | tf_op jit(solution)/shard_map/ppermute | solution.py:325
  12.3 2.5 %collective-permute-start.4 = (f32[1032,128]{1,0:T(8,128)S(1)}, f32[1032,128]{1,0:T(8,128)S(1)}, u32[]{:S(2)}, u32[]{:S(2)}) collective-permute-start(f32[1032,128]{1,0:T(8,128)S(1)} %get-tuple-element.36.zb), channel_id=1, source_target_pairs={{0,32},{1,2},{2,1},{3,4},{4,3},{5,6},{6,5},{7,39},{32,0},{33,34},{... | collective-permute-start | bytes 1585160 | tf_op jit(solution)/shard_map/ppermute | solution.py:343
  14.7 2.7 %sides.1 = (bf16[1536,512]{1,0:T(8,128)(2,1)S(1)}, f32[512,128]{1,0:T(8,128)S(1)}, f32[512,128]{1,0:T(8,128)S(1)}, f32[128,128]{1,0:T(8,128)S(1)}, f32[128,128]{1,0:T(8,128)S(1)}, /*index=5*/f32[1024,128]{1,0:T(8,128)S(1)}) custom-call(bf16[9216,128]{1,0:T(8,128)(2,1)S(1)} %get-tuple-element.25.sall, bf16[1536,1536]{1,0:T(8,128)(2,1)S(1)} %get-tuple-element.26.lbuf, ...), custom_call_target="tpu_custom_call" | custom-call | flops 3000000000 | bytes 1000000 | tf_op jit(solution)/shard_map/sides/pallas_call | solution.py:427
  17.4 0.1 collective-permute-start.7
  17.5 0.1 collective-permute-start.5
  17.6 1.9 %collective-permute-start.6 = (f32[512,128]{1,0:T(8,128)S(1)}, f32[512,128]{1,0:T(8,128)S(1)}, u32[]{:S(2)}, u32[]{:S(2)}) collective-permute-start(f32[512,128]{1,0:T(8,128)S(1)} %get-tuple-element.38.yeb), channel_id=1, source_target_pairs={{0,32},{8,16},{16,8},{24,56},{32,0},{40,48},{48,40},{56,24},{64,96... | collective-permute-start | bytes 786440 | tf_op jit(solution)/shard_map/ppermute | solution.py:343
  19.5 0.0 collective-permute-done.7.fxa
  19.5 0.3 collective-permute-start.2
  19.7 3.5 %rest.1.before = f32[1536,1536]{1,0:T(8,128)} custom-call(s32[8,128]{1,0:T(8,128)S(1)} %get-tuple-element.24.spots, bf16[9216,128]{1,0:T(8,128)(2,1)S(1)} %get-tuple-element.25.sall, bf16[1536,512]{1,0:T(8,128)(2,1)S(1)} %get-tuple-element.28.wbd, bf16[1536,512]{1,0:T(8,128)(2,1)S(1)} %get-tuple-element.40.wac, bf16[1536,512]{1,0:T(8,128)(2,1)S(1)} %get-tuple-element.41.wef, ...), custom_call_target="tpu_custom_call" | custom-call | flops 3000000000 | bytes 8000000 | tf_op jit(solution)/shard_map/rest/pallas_call | solution.py:447
  23.3 2.9 %collective-permute-done.5.fyea = f32[512,128]{1,0:T(8,128)S(1)} collective-permute-done((f32[512,128]{1,0:T(8,128)S(1)}, f32[512,128]{1,0:T(8,128)S(1)}, u32[]{:S(2)}, u32[]{:S(2)}) %collective-permute-start.5) | collective-permute-done | bytes 262176 | tf_op jit(solution)/shard_map/ppermute | solution.py:325
  26.2 0.1 collective-permute-done.6.fyeb
  26.3 1.1 %borders.1.before = f32[1536,1536]{1,0:T(8,128)} custom-call(s32[8,128]{1,0:T(8,128)S(1)} %get-tuple-element.24.spots, f32[512,128]{1,0:T(8,128)S(1)} %get-tuple-element.37.yea, f32[512,128]{1,0:T(8,128)S(1)} %get-tuple-element.38.yeb, f32[512,128]{1,0:T(8,128)S(1)} %collective-permute-done.5.fyea, ...), custom_call_target="tpu_custom_call", output_to_operand_aliasing={{}: (7, {})} | custom-call | flops 100000000 | bytes 1000000 | tf_op jit(solution)/shard_map/borders/pallas_call | solution.py:461
  27.3 0.0 collective-permute-done.3.fza
  27.4 2.1 %collective-permute-done.4.fzb = f32[1032,128]{1,0:T(8,128)S(1)} collective-permute-done((f32[1032,128]{1,0:T(8,128)S(1)}, f32[1032,128]{1,0:T(8,128)S(1)}, u32[]{:S(2)}, u32[]{:S(2)}) %collective-permute-start.4) | collective-permute-done | bytes 528416 | tf_op jit(solution)/shard_map/ppermute | solution.py:343
  29.5 1.4 %last.1.before = f32[1536,1536]{1,0:T(8,128)} custom-call(s32[8,128]{1,0:T(8,128)S(1)} %get-tuple-element.24.spots, f32[1032,128]{1,0:T(8,128)S(1)} %get-tuple-element.34.after.za, f32[1032,128]{1,0:T(8,128)S(1)} %get-tuple-element.36.zb, f32[1032,128]{1,0:T(8,128)S(1)} %collective-permute-done.3.fza, ...), custom_call_target="tpu_custom_call", output_to_operand_aliasing={{}: (5, {})} | custom-call | flops 100000000 | bytes 2000000 | tf_op jit(solution)/shard_map/last/pallas_call | solution.py:472
  30.9 0.0 collective-permute-done.2.fxb
  30.9 0.7 %end.1 = f32[1536,1536]{1,0:T(8,128)} custom-call(s32[8,128]{1,0:T(8,128)S(1)} %get-tuple-element.24.spots, f32[128,128]{1,0:T(8,128)S(1)} %get-tuple-element.35.xb, f32[128,128]{1,0:T(8,128)S(1)} %collective-permute-done.2.fxb, f32[1536,1536]{1,0:T(8,128)} %last.1.before), custom_call_target="tpu_custom_call", output_to_operand_aliasing={{}: (3, {})} | custom-call | flops 10000000 | bytes 100000 | tf_op jit(solution)/shard_map/end/pallas_call | solution.py:483
  (1 shorter events, 0.0 us)
Async XLA Ops:
  4.8 5.4 %collective-permute-start = (f32[136,128]{1,0:T(8,128)S(1)}, f32[136,128]{1,0:T(8,128)S(1)}, u32[]{:S(2)}, u32[]{:S(2)}) collective-permute-start(f32[136,128]{1,0:T(8,128)S(1)} %get-tuple-element.32), channel_id=1, source_target_pairs={{0,8},{8,0},{16,24},{24,16},{1,9},{9,1},{17,25},{25,17},{2,10},{10... | collective-permute-start | bytes 208904 | tf_op jit(solution)/shard_map/ppermute | solution.py:325
  5.3 4.9 %collective-permute-start.1 = (f32[136,128]{1,0:T(8,128)S(1)}, f32[136,128]{1,0:T(8,128)S(1)}, u32[]{:S(2)}, u32[]{:S(2)}) collective-permute-start(f32[136,128]{1,0:T(8,128)S(1)} %get-tuple-element.33), channel_id=1, source_target_pairs={{0,32},{8,16},{16,8},{24,56},{32,0},{40,48},{48,40},{56,24},{64,96... | collective-permute-start | bytes 208904 | tf_op jit(solution)/shard_map/ppermute | solution.py:343
  10.3 17.1 %collective-permute-start.3 = (f32[1032,128]{1,0:T(8,128)S(1)}, f32[1032,128]{1,0:T(8,128)S(1)}, u32[]{:S(2)}, u32[]{:S(2)}) collective-permute-start(f32[1032,128]{1,0:T(8,128)S(1)} %get-tuple-element.34.after.za), channel_id=1, source_target_pairs={{0,1},{1,0},{2,3},{3,2},{4,5},{5,4},{6,7},{7,6},{8,9},{9,8},{10,11... | collective-permute-start | bytes 1585160 | tf_op jit(solution)/shard_map/ppermute | solution.py:325
  12.3 17.2 %collective-permute-start.4 = (f32[1032,128]{1,0:T(8,128)S(1)}, f32[1032,128]{1,0:T(8,128)S(1)}, u32[]{:S(2)}, u32[]{:S(2)}) collective-permute-start(f32[1032,128]{1,0:T(8,128)S(1)} %get-tuple-element.36.zb), channel_id=1, source_target_pairs={{0,32},{1,2},{2,1},{3,4},{4,3},{5,6},{6,5},{7,39},{32,0},{33,34},{... | collective-permute-start | bytes 1585160 | tf_op jit(solution)/shard_map/ppermute | solution.py:343
  17.4 2.1 %collective-permute-start.7 = (f32[128,128]{1,0:T(8,128)S(1)}, f32[128,128]{1,0:T(8,128)S(1)}, u32[]{:S(2)}, u32[]{:S(2)}) collective-permute-start(f32[128,128]{1,0:T(8,128)S(1)} %get-tuple-element.39.xa), channel_id=1, source_target_pairs={{0,32},{32,0},{64,96},{96,64},{1,33},{33,1},{65,97},{97,65},{2,34}... | collective-permute-start | bytes 196616 | tf_op jit(solution)/shard_map/ppermute | solution.py:325
  17.5 8.7 %collective-permute-start.5 = (f32[512,128]{1,0:T(8,128)S(1)}, f32[512,128]{1,0:T(8,128)S(1)}, u32[]{:S(2)}, u32[]{:S(2)}) collective-permute-start(f32[512,128]{1,0:T(8,128)S(1)} %get-tuple-element.37.yea), channel_id=1, source_target_pairs={{0,8},{8,0},{16,24},{24,16},{1,9},{9,1},{17,25},{25,17},{2,10},{10... | collective-permute-start | bytes 786440 | tf_op jit(solution)/shard_map/ppermute | solution.py:325
  17.6 8.7 %collective-permute-start.6 = (f32[512,128]{1,0:T(8,128)S(1)}, f32[512,128]{1,0:T(8,128)S(1)}, u32[]{:S(2)}, u32[]{:S(2)}) collective-permute-start(f32[512,128]{1,0:T(8,128)S(1)} %get-tuple-element.38.yeb), channel_id=1, source_target_pairs={{0,32},{8,16},{16,8},{24,56},{32,0},{40,48},{48,40},{56,24},{64,96... | collective-permute-start | bytes 786440 | tf_op jit(solution)/shard_map/ppermute | solution.py:343
  19.5 11.4 %collective-permute-start.2 = (f32[128,128]{1,0:T(8,128)S(1)}, f32[128,128]{1,0:T(8,128)S(1)}, u32[]{:S(2)}, u32[]{:S(2)}) collective-permute-start(f32[128,128]{1,0:T(8,128)S(1)} %get-tuple-element.35.xb), channel_id=1, source_target_pairs={{0,8},{8,0},{16,24},{24,16},{32,64},{40,72},{48,80},{56,88},{64,32... | collective-permute-start | bytes 196616 | tf_op jit(solution)/shard_map/ppermute | solution.py:337
